TPU v7x, 32 devices: a whole 2x2x4 slice. The times are simulated.
32 devices in a mesh: mkt: 8 (over y, x, core), trade: 1, scen: 4 (over z).
Axes of the slice: x: 2, y: 2, z: 4, core: 2. Of those that a mesh axis runs over, the one named last changes fastest.
Arguments:
- quotes: bfloat16 [512, 512], P('mkt'), may hold values from -6 to 6
- kernel: bfloat16 [64, 128, 128], P(('trade', 'scen')), may hold values from -0.5 to 0.5
- trade_block: int32 [2048], P('trade'), may hold values from 0 to 63
- trade_embed: bfloat16 [2048, 256], P('trade'), may hold values from -6 to 6
- position: float32 [2048], P('trade'), may hold values from -0.125 to 0.125
- scen_rank: int32 [512], P(('mkt', 'scen')), may hold values from 0 to 511, each once
- w_in: bfloat16 [128, 256], replicated, may hold values from -0.5 to 0.5
- w_mid: bfloat16 [256, 256], replicated, may hold values from -0.375 to 0.375
- b_mid: float32 [256], replicated, may hold values from -6 to 6
- w_out: bfloat16 [256], replicated, may hold values from -0.375 to 0.375
Outputs:
- book_pnl: float32 [512], P(('mkt', 'scen'))
- marginal: float32 [2048], P('trade')
- shortfall: float32 [], replicated
Inputs may be any that keep to these rules, and one draw needn't show every extreme that they name: scen_rank holds each rank of 0 to 511 once.
All inputs are finite; a program needn't handle non-finite values.
Results may differ from a plain program's by a relative error of at most 0.014.
The roundings to bfloat16 on the way count: a program that leaves them out, or rounds other values in their place, can miss the bound.
Values may be sent and summed in bfloat16 or wider, within the bound.
No kernel may reach another device: no remote copies, remote signals or barrier semaphores. Data moves between devices by JAX's collectives and lax.ppermute only.
A program may use at most 64 MiB of HBM per device.

v0:
```python
import jax
import jax.numpy as jnp
from jax import lax
from jax.sharding import PartitionSpec as P

SEG = 128
WIN = 128
QSTEP = 8


def local(quotes, kernel, trade_block, trade_embed, position, scen_rank, w_in, w_mid, b_mid, w_out):
    local_count = kernel.shape[0]
    quote_count = quotes.shape[1]
    row_count = quotes.shape[0]
    first_block = lax.axis_index(("trade", "scen")) * local_count

    def cut_window(local_block):
        block_index = first_block + local_block
        window_start = jnp.clip(QSTEP * block_index - (WIN - QSTEP) // 2, 0, quote_count - WIN)
        return lax.dynamic_slice_in_dim(quotes, window_start, WIN, 1)

    windows = jax.vmap(cut_window)(jnp.arange(local_count, dtype=jnp.int32))
    built_state = jnp.einsum("jrw,jws->jrs", windows, kernel, preferred_element_type=jnp.float32)
    built_state = built_state.astype(jnp.bfloat16).reshape(local_count, row_count * SEG)
    scen_count = scen_rank.shape[0]
    quarter = lax.all_to_all(built_state, "scen", split_axis=1, concat_axis=0, tiled=True)
    table = lax.all_gather(quarter, "trade", axis=0, tiled=True)
    trade_rows_all = table[trade_block]
    embed_float = trade_embed.astype(jnp.float32)

    def price(scen_index):
        trade_rows = lax.dynamic_slice_in_dim(trade_rows_all, scen_index * SEG, SEG, 1)
        hidden_one = jax.nn.silu(
            jnp.dot(trade_rows, w_in, preferred_element_type=jnp.float32) + embed_float
        ).astype(jnp.bfloat16)
        hidden_two = jax.nn.silu(
            jnp.dot(hidden_one, w_mid, preferred_element_type=jnp.float32) + b_mid
        ).astype(jnp.bfloat16)
        return jnp.dot(hidden_two, w_out, preferred_element_type=jnp.float32)

    values = lax.map(price, jnp.arange(scen_count, dtype=jnp.int32))
    scen_total = scen_count * lax.axis_size("mkt") * lax.axis_size("scen")
    decay_span = scen_total // 20
    weight_sum = jnp.sum(jnp.exp(-jnp.arange(scen_total, dtype=jnp.float32) / decay_span))
    weights = jnp.exp(-scen_rank.astype(jnp.float32) / decay_span) / weight_sum
    pnl_part = jnp.dot(values, position, precision=lax.Precision.HIGHEST)
    marginal = lax.psum(-jnp.dot(weights, values, precision=lax.Precision.HIGHEST), ("mkt", "scen"))
    book_pnl = lax.psum(pnl_part, "trade")
    local_tail = -jnp.dot(weights, book_pnl, precision=lax.Precision.HIGHEST)
    shortfall = lax.psum(local_tail, ("mkt", "scen"))
    return (book_pnl, marginal, shortfall)


def solution(mesh):
    placed = (
        P("mkt", None),
        P(("trade", "scen"), None, None),
        P("trade"),
        P("trade", None),
        P("trade"),
        P(("mkt", "scen")),
        P(),
        P(),
        P(),
        P(),
    )
    return jax.shard_map(
        local,
        mesh=mesh,
        in_specs=placed,
        out_specs=(P(("mkt", "scen")), P("trade"), P()),
        check_vma=False,
    )
```

profile of v0, /device:TPU:0, one launch (start us, length us, event | category | flops | bytes accessed | tf_op | source)
XLA Modules:
  0.0 204.2 jit_solution(12396054698393962323)
XLA Ops:
  0.7 33.3 %while.12 = (s32[]{:T(128)}, bf16[64,512]{1,0:T(8,128)(2,1)}, s32[16,2]{0,1:T(2,128)S(1)}, bf16[16,64,128]{2,1,0:T(8,128)(2,1)S(1)}, s32[]{:T(128)}) while((s32[]{:T(128)}, bf16[64,512]{1,0:T(8,128)(2,1)}, s32[16,2]{0,1:T(2,128)S(1)}, bf16[16,64,128]{2,1,0:T(8,128)(2,1)S(1)}, s32[]{:T(128)}) %tuple.34), condition=%wide.while_cond, body=%wide.while_body.sunk | while | flops 2 | bytes 32865 | solution.py:20
  1.3 1.5 bitcast_dynamic-update-slice_fusion.2
  3.4 1.5 bitcast_dynamic-update-slice_fusion.2
  5.5 1.5 bitcast_dynamic-update-slice_fusion.2
  7.5 1.5 bitcast_dynamic-update-slice_fusion.2
  9.6 1.5 bitcast_dynamic-update-slice_fusion.2
  11.7 1.5 bitcast_dynamic-update-slice_fusion.2
  13.8 1.5 bitcast_dynamic-update-slice_fusion.2
  15.9 1.5 bitcast_dynamic-update-slice_fusion.2
  17.9 1.5 bitcast_dynamic-update-slice_fusion.2
  20.0 1.5 bitcast_dynamic-update-slice_fusion.2
  22.1 1.5 bitcast_dynamic-update-slice_fusion.2
  24.2 1.5 bitcast_dynamic-update-slice_fusion.2
  26.3 1.5 bitcast_dynamic-update-slice_fusion.2
  28.3 1.5 bitcast_dynamic-update-slice_fusion.2
  30.4 1.5 bitcast_dynamic-update-slice_fusion.2
  32.5 1.5 bitcast_dynamic-update-slice_fusion.2
  34.4 0.8 copy.14
  35.2 6.0 %all-to-all-start = ((bf16[16,4,2048]{2,0,1:T(8,128)(2,1)}), bf16[16,4,2048]{2,0,1:T(8,128)(2,1)S(1)}, u32[]{:S(2)}, u32[]{:S(2)}) async-start(bf16[16,4,2048]{2,0,1:T(8,128)(2,1)} %copy.14), calls=%async_computation | async-start | bytes 524288 | tf_op jit(solution)/shard_map/all_to_all | solution.py:26
  41.2 1.4 convert_element_type.16
  42.6 0.6 exponential_reduce_fusion
  43.2 6.9 %all-to-all-done = bf16[16,4,2048]{2,0,1:T(8,128)(2,1)S(1)} async-done(((bf16[16,4,2048]{2,0,1:T(8,128)(2,1)}), bf16[16,4,2048]{2,0,1:T(8,128)(2,1)S(1)}, u32[]{:S(2)}, u32[]{:S(2)}) %all-to-all-start) | async-done | bytes 262176 | tf_op jit(solution)/shard_map/all_to_all | solution.py:26
  50.2 11.0 %gather_fusion = bf16[2048,2048]{1,0:T(8,128)(2,1)} fusion(bf16[64,2048]{1,0:T(8,128)(2,1)S(1)} %bitcast.38, s32[2048]{0:T(1024)S(1)} %fusion.6), kind=kCustom, calls=%fused_computation | custom fusion | bytes 16785408 | tf_op jit(solution)/shard_map/gather | solution.py:28
  61.2 100.5 %while.11 = (s32[]{:T(128)}, f32[16,2048]{1,0:T(8,128)S(1)}, s32[16]{0:T(128)S(1)}, bf16[2048,2048]{1,0:T(8,128)(2,1)}, bf16[128,256]{1,0:T(8,128)(2,1)S(1)}, /*...) while((s32[]{:T(128)}, f32[16,2048]{1,0:T(8,128)S(1)}, ...), condition=%wide.region_1.2_spmd, body=%wide.region_0.1_spmd.sunk | while | flops 409993216 | bytes 4942527 | solution.py:41
  61.2 0.6 dynamic_slice.12
  62.4 2.8 %multiply_convert_fusion.3 = bf16[2048,256]{1,0:T(8,128)(2,1)} fusion(f32[2048,256]{1,0:T(8,128)S(1)} %get-tuple-element.215, bf16[128,256]{1,0:T(8,128)(2,1)S(1)} %get-tuple-element.214, bf16[2048,2048]{1,0:T(8,128)(2,1)} %get-tuple-element.213, s32[]{:T(128)S(6)} %select_n.23), kind=kOutput, calls=%fused_computation.4.clone.1 | convolution fusion | flops 137363456 | bytes 3735556 | tf_op jit(solution)/shard_map/while/body/eval_jaxpr/dot_general | solution.py:34
  65.2 2.0 %fusion.29 = f32[1,2048]{1,0:T(1,128)S(1)} fusion(bf16[256,1]{0,1:T(2,128)(2,1)S(1)} %reshape.77, bf16[2048,256]{1,0:T(8,128)(2,1)} %multiply_convert_fusion.3, bf16[256,256]{1,0:T(8,128)(2,1)S(1)} %get-tuple-element.216, f32[256]{0:T(256)S(1)} %get-tuple-element.217), kind=kOutput, calls=%fused_computation.5.clone.1 | convolution fusion | flops 272629760 | bytes 1189376 | tf_op jit(solution)/shard_map/while/body/eval_jaxpr/dot_general | solution.py:39
  68.7 2.8 %multiply_convert_fusion.3 = bf16[2048,256]{1,0:T(8,128)(2,1)} fusion(f32[2048,256]{1,0:T(8,128)S(1)} %get-tuple-element.215, bf16[128,256]{1,0:T(8,128)(2,1)S(1)} %get-tuple-element.214, bf16[2048,2048]{1,0:T(8,128)(2,1)} %get-tuple-element.213, s32[]{:T(128)S(6)} %select_n.23), kind=kOutput, calls=%fused_computation.4.clone.1 | convolution fusion | flops 137363456 | bytes 3735556 | tf_op jit(solution)/shard_map/while/body/eval_jaxpr/dot_general | solution.py:34
  71.5 2.0 %fusion.29 = f32[1,2048]{1,0:T(1,128)S(1)} fusion(bf16[256,1]{0,1:T(2,128)(2,1)S(1)} %reshape.77, bf16[2048,256]{1,0:T(8,128)(2,1)} %multiply_convert_fusion.3, bf16[256,256]{1,0:T(8,128)(2,1)S(1)} %get-tuple-element.216, f32[256]{0:T(256)S(1)} %get-tuple-element.217), kind=kOutput, calls=%fused_computation.5.clone.1 | convolution fusion | flops 272629760 | bytes 1189376 | tf_op jit(solution)/shard_map/while/body/eval_jaxpr/dot_general | solution.py:39
  75.0 2.8 %multiply_convert_fusion.3 = bf16[2048,256]{1,0:T(8,128)(2,1)} fusion(f32[2048,256]{1,0:T(8,128)S(1)} %get-tuple-element.215, bf16[128,256]{1,0:T(8,128)(2,1)S(1)} %get-tuple-element.214, bf16[2048,2048]{1,0:T(8,128)(2,1)} %get-tuple-element.213, s32[]{:T(128)S(6)} %select_n.23), kind=kOutput, calls=%fused_computation.4.clone.1 | convolution fusion | flops 137363456 | bytes 3735556 | tf_op jit(solution)/shard_map/while/body/eval_jaxpr/dot_general | solution.py:34
  77.8 2.0 %fusion.29 = f32[1,2048]{1,0:T(1,128)S(1)} fusion(bf16[256,1]{0,1:T(2,128)(2,1)S(1)} %reshape.77, bf16[2048,256]{1,0:T(8,128)(2,1)} %multiply_convert_fusion.3, bf16[256,256]{1,0:T(8,128)(2,1)S(1)} %get-tuple-element.216, f32[256]{0:T(256)S(1)} %get-tuple-element.217), kind=kOutput, calls=%fused_computation.5.clone.1 | convolution fusion | flops 272629760 | bytes 1189376 | tf_op jit(solution)/shard_map/while/body/eval_jaxpr/dot_general | solution.py:39
  81.3 2.8 %multiply_convert_fusion.3 = bf16[2048,256]{1,0:T(8,128)(2,1)} fusion(f32[2048,256]{1,0:T(8,128)S(1)} %get-tuple-element.215, bf16[128,256]{1,0:T(8,128)(2,1)S(1)} %get-tuple-element.214, bf16[2048,2048]{1,0:T(8,128)(2,1)} %get-tuple-element.213, s32[]{:T(128)S(6)} %select_n.23), kind=kOutput, calls=%fused_computation.4.clone.1 | convolution fusion | flops 137363456 | bytes 3735556 | tf_op jit(solution)/shard_map/while/body/eval_jaxpr/dot_general | solution.py:34
  84.1 2.0 %fusion.29 = f32[1,2048]{1,0:T(1,128)S(1)} fusion(bf16[256,1]{0,1:T(2,128)(2,1)S(1)} %reshape.77, bf16[2048,256]{1,0:T(8,128)(2,1)} %multiply_convert_fusion.3, bf16[256,256]{1,0:T(8,128)(2,1)S(1)} %get-tuple-element.216, f32[256]{0:T(256)S(1)} %get-tuple-element.217), kind=kOutput, calls=%fused_computation.5.clone.1 | convolution fusion | flops 272629760 | bytes 1189376 | tf_op jit(solution)/shard_map/while/body/eval_jaxpr/dot_general | solution.py:39
  86.3 0.6 dynamic_slice.12
  87.6 2.8 %multiply_convert_fusion.3 = bf16[2048,256]{1,0:T(8,128)(2,1)} fusion(f32[2048,256]{1,0:T(8,128)S(1)} %get-tuple-element.215, bf16[128,256]{1,0:T(8,128)(2,1)S(1)} %get-tuple-element.214, bf16[2048,2048]{1,0:T(8,128)(2,1)} %get-tuple-element.213, s32[]{:T(128)S(6)} %select_n.23), kind=kOutput, calls=%fused_computation.4.clone.1 | convolution fusion | flops 137363456 | bytes 3735556 | tf_op jit(solution)/shard_map/while/body/eval_jaxpr/dot_general | solution.py:34
  90.4 2.0 %fusion.29 = f32[1,2048]{1,0:T(1,128)S(1)} fusion(bf16[256,1]{0,1:T(2,128)(2,1)S(1)} %reshape.77, bf16[2048,256]{1,0:T(8,128)(2,1)} %multiply_convert_fusion.3, bf16[256,256]{1,0:T(8,128)(2,1)S(1)} %get-tuple-element.216, f32[256]{0:T(256)S(1)} %get-tuple-element.217), kind=kOutput, calls=%fused_computation.5.clone.1 | convolution fusion | flops 272629760 | bytes 1189376 | tf_op jit(solution)/shard_map/while/body/eval_jaxpr/dot_general | solution.py:39
  92.6 0.6 dynamic_slice.12
  93.8 2.8 %multiply_convert_fusion.3 = bf16[2048,256]{1,0:T(8,128)(2,1)} fusion(f32[2048,256]{1,0:T(8,128)S(1)} %get-tuple-element.215, bf16[128,256]{1,0:T(8,128)(2,1)S(1)} %get-tuple-element.214, bf16[2048,2048]{1,0:T(8,128)(2,1)} %get-tuple-element.213, s32[]{:T(128)S(6)} %select_n.23), kind=kOutput, calls=%fused_computation.4.clone.1 | convolution fusion | flops 137363456 | bytes 3735556 | tf_op jit(solution)/shard_map/while/body/eval_jaxpr/dot_general | solution.py:34
  96.6 2.0 %fusion.29 = f32[1,2048]{1,0:T(1,128)S(1)} fusion(bf16[256,1]{0,1:T(2,128)(2,1)S(1)} %reshape.77, bf16[2048,256]{1,0:T(8,128)(2,1)} %multiply_convert_fusion.3, bf16[256,256]{1,0:T(8,128)(2,1)S(1)} %get-tuple-element.216, f32[256]{0:T(256)S(1)} %get-tuple-element.217), kind=kOutput, calls=%fused_computation.5.clone.1 | convolution fusion | flops 272629760 | bytes 1189376 | tf_op jit(solution)/shard_map/while/body/eval_jaxpr/dot_general | solution.py:39
  100.1 2.8 %multiply_convert_fusion.3 = bf16[2048,256]{1,0:T(8,128)(2,1)} fusion(f32[2048,256]{1,0:T(8,128)S(1)} %get-tuple-element.215, bf16[128,256]{1,0:T(8,128)(2,1)S(1)} %get-tuple-element.214, bf16[2048,2048]{1,0:T(8,128)(2,1)} %get-tuple-element.213, s32[]{:T(128)S(6)} %select_n.23), kind=kOutput, calls=%fused_computation.4.clone.1 | convolution fusion | flops 137363456 | bytes 3735556 | tf_op jit(solution)/shard_map/while/body/eval_jaxpr/dot_general | solution.py:34
  102.9 2.0 %fusion.29 = f32[1,2048]{1,0:T(1,128)S(1)} fusion(bf16[256,1]{0,1:T(2,128)(2,1)S(1)} %reshape.77, bf16[2048,256]{1,0:T(8,128)(2,1)} %multiply_convert_fusion.3, bf16[256,256]{1,0:T(8,128)(2,1)S(1)} %get-tuple-element.216, f32[256]{0:T(256)S(1)} %get-tuple-element.217), kind=kOutput, calls=%fused_computation.5.clone.1 | convolution fusion | flops 272629760 | bytes 1189376 | tf_op jit(solution)/shard_map/while/body/eval_jaxpr/dot_general | solution.py:39
  106.4 2.8 %multiply_convert_fusion.3 = bf16[2048,256]{1,0:T(8,128)(2,1)} fusion(f32[2048,256]{1,0:T(8,128)S(1)} %get-tuple-element.215, bf16[128,256]{1,0:T(8,128)(2,1)S(1)} %get-tuple-element.214, bf16[2048,2048]{1,0:T(8,128)(2,1)} %get-tuple-element.213, s32[]{:T(128)S(6)} %select_n.23), kind=kOutput, calls=%fused_computation.4.clone.1 | convolution fusion | flops 137363456 | bytes 3735556 | tf_op jit(solution)/shard_map/while/body/eval_jaxpr/dot_general | solution.py:34
  109.2 2.0 %fusion.29 = f32[1,2048]{1,0:T(1,128)S(1)} fusion(bf16[256,1]{0,1:T(2,128)(2,1)S(1)} %reshape.77, bf16[2048,256]{1,0:T(8,128)(2,1)} %multiply_convert_fusion.3, bf16[256,256]{1,0:T(8,128)(2,1)S(1)} %get-tuple-element.216, f32[256]{0:T(256)S(1)} %get-tuple-element.217), kind=kOutput, calls=%fused_computation.5.clone.1 | convolution fusion | flops 272629760 | bytes 1189376 | tf_op jit(solution)/shard_map/while/body/eval_jaxpr/dot_general | solution.py:39
  111.4 0.6 dynamic_slice.12
  112.7 2.8 %multiply_convert_fusion.3 = bf16[2048,256]{1,0:T(8,128)(2,1)} fusion(f32[2048,256]{1,0:T(8,128)S(1)} %get-tuple-element.215, bf16[128,256]{1,0:T(8,128)(2,1)S(1)} %get-tuple-element.214, bf16[2048,2048]{1,0:T(8,128)(2,1)} %get-tuple-element.213, s32[]{:T(128)S(6)} %select_n.23), kind=kOutput, calls=%fused_computation.4.clone.1 | convolution fusion | flops 137363456 | bytes 3735556 | tf_op jit(solution)/shard_map/while/body/eval_jaxpr/dot_general | solution.py:34
  115.5 2.0 %fusion.29 = f32[1,2048]{1,0:T(1,128)S(1)} fusion(bf16[256,1]{0,1:T(2,128)(2,1)S(1)} %reshape.77, bf16[2048,256]{1,0:T(8,128)(2,1)} %multiply_convert_fusion.3, bf16[256,256]{1,0:T(8,128)(2,1)S(1)} %get-tuple-element.216, f32[256]{0:T(256)S(1)} %get-tuple-element.217), kind=kOutput, calls=%fused_computation.5.clone.1 | convolution fusion | flops 272629760 | bytes 1189376 | tf_op jit(solution)/shard_map/while/body/eval_jaxpr/dot_general | solution.py:39
  117.7 0.6 dynamic_slice.12
  119.0 2.8 %multiply_convert_fusion.3 = bf16[2048,256]{1,0:T(8,128)(2,1)} fusion(f32[2048,256]{1,0:T(8,128)S(1)} %get-tuple-element.215, bf16[128,256]{1,0:T(8,128)(2,1)S(1)} %get-tuple-element.214, bf16[2048,2048]{1,0:T(8,128)(2,1)} %get-tuple-element.213, s32[]{:T(128)S(6)} %select_n.23), kind=kOutput, calls=%fused_computation.4.clone.1 | convolution fusion | flops 137363456 | bytes 3735556 | tf_op jit(solution)/shard_map/while/body/eval_jaxpr/dot_general | solution.py:34
  121.8 2.0 %fusion.29 = f32[1,2048]{1,0:T(1,128)S(1)} fusion(bf16[256,1]{0,1:T(2,128)(2,1)S(1)} %reshape.77, bf16[2048,256]{1,0:T(8,128)(2,1)} %multiply_convert_fusion.3, bf16[256,256]{1,0:T(8,128)(2,1)S(1)} %get-tuple-element.216, f32[256]{0:T(256)S(1)} %get-tuple-element.217), kind=kOutput, calls=%fused_computation.5.clone.1 | convolution fusion | flops 272629760 | bytes 1189376 | tf_op jit(solution)/shard_map/while/body/eval_jaxpr/dot_general | solution.py:39
  125.2 2.8 %multiply_convert_fusion.3 = bf16[2048,256]{1,0:T(8,128)(2,1)} fusion(f32[2048,256]{1,0:T(8,128)S(1)} %get-tuple-element.215, bf16[128,256]{1,0:T(8,128)(2,1)S(1)} %get-tuple-element.214, bf16[2048,2048]{1,0:T(8,128)(2,1)} %get-tuple-element.213, s32[]{:T(128)S(6)} %select_n.23), kind=kOutput, calls=%fused_computation.4.clone.1 | convolution fusion | flops 137363456 | bytes 3735556 | tf_op jit(solution)/shard_map/while/body/eval_jaxpr/dot_general | solution.py:34
  128.0 2.0 %fusion.29 = f32[1,2048]{1,0:T(1,128)S(1)} fusion(bf16[256,1]{0,1:T(2,128)(2,1)S(1)} %reshape.77, bf16[2048,256]{1,0:T(8,128)(2,1)} %multiply_convert_fusion.3, bf16[256,256]{1,0:T(8,128)(2,1)S(1)} %get-tuple-element.216, f32[256]{0:T(256)S(1)} %get-tuple-element.217), kind=kOutput, calls=%fused_computation.5.clone.1 | convolution fusion | flops 272629760 | bytes 1189376 | tf_op jit(solution)/shard_map/while/body/eval_jaxpr/dot_general | solution.py:39
  131.5 2.8 %multiply_convert_fusion.3 = bf16[2048,256]{1,0:T(8,128)(2,1)} fusion(f32[2048,256]{1,0:T(8,128)S(1)} %get-tuple-element.215, bf16[128,256]{1,0:T(8,128)(2,1)S(1)} %get-tuple-element.214, bf16[2048,2048]{1,0:T(8,128)(2,1)} %get-tuple-element.213, s32[]{:T(128)S(6)} %select_n.23), kind=kOutput, calls=%fused_computation.4.clone.1 | convolution fusion | flops 137363456 | bytes 3735556 | tf_op jit(solution)/shard_map/while/body/eval_jaxpr/dot_general | solution.py:34
  134.3 2.0 %fusion.29 = f32[1,2048]{1,0:T(1,128)S(1)} fusion(bf16[256,1]{0,1:T(2,128)(2,1)S(1)} %reshape.77, bf16[2048,256]{1,0:T(8,128)(2,1)} %multiply_convert_fusion.3, bf16[256,256]{1,0:T(8,128)(2,1)S(1)} %get-tuple-element.216, f32[256]{0:T(256)S(1)} %get-tuple-element.217), kind=kOutput, calls=%fused_computation.5.clone.1 | convolution fusion | flops 272629760 | bytes 1189376 | tf_op jit(solution)/shard_map/while/body/eval_jaxpr/dot_general | solution.py:39
  137.8 2.8 %multiply_convert_fusion.3 = bf16[2048,256]{1,0:T(8,128)(2,1)} fusion(f32[2048,256]{1,0:T(8,128)S(1)} %get-tuple-element.215, bf16[128,256]{1,0:T(8,128)(2,1)S(1)} %get-tuple-element.214, bf16[2048,2048]{1,0:T(8,128)(2,1)} %get-tuple-element.213, s32[]{:T(128)S(6)} %select_n.23), kind=kOutput, calls=%fused_computation.4.clone.1 | convolution fusion | flops 137363456 | bytes 3735556 | tf_op jit(solution)/shard_map/while/body/eval_jaxpr/dot_general | solution.py:34
  140.6 2.0 %fusion.29 = f32[1,2048]{1,0:T(1,128)S(1)} fusion(bf16[256,1]{0,1:T(2,128)(2,1)S(1)} %reshape.77, bf16[2048,256]{1,0:T(8,128)(2,1)} %multiply_convert_fusion.3, bf16[256,256]{1,0:T(8,128)(2,1)S(1)} %get-tuple-element.216, f32[256]{0:T(256)S(1)} %get-tuple-element.217), kind=kOutput, calls=%fused_computation.5.clone.1 | convolution fusion | flops 272629760 | bytes 1189376 | tf_op jit(solution)/shard_map/while/body/eval_jaxpr/dot_general | solution.py:39
  144.1 2.8 %multiply_convert_fusion.3 = bf16[2048,256]{1,0:T(8,128)(2,1)} fusion(f32[2048,256]{1,0:T(8,128)S(1)} %get-tuple-element.215, bf16[128,256]{1,0:T(8,128)(2,1)S(1)} %get-tuple-element.214, bf16[2048,2048]{1,0:T(8,128)(2,1)} %get-tuple-element.213, s32[]{:T(128)S(6)} %select_n.23), kind=kOutput, calls=%fused_computation.4.clone.1 | convolution fusion | flops 137363456 | bytes 3735556 | tf_op jit(solution)/shard_map/while/body/eval_jaxpr/dot_general | solution.py:34
  146.9 2.0 %fusion.29 = f32[1,2048]{1,0:T(1,128)S(1)} fusion(bf16[256,1]{0,1:T(2,128)(2,1)S(1)} %reshape.77, bf16[2048,256]{1,0:T(8,128)(2,1)} %multiply_convert_fusion.3, bf16[256,256]{1,0:T(8,128)(2,1)S(1)} %get-tuple-element.216, f32[256]{0:T(256)S(1)} %get-tuple-element.217), kind=kOutput, calls=%fused_computation.5.clone.1 | convolution fusion | flops 272629760 | bytes 1189376 | tf_op jit(solution)/shard_map/while/body/eval_jaxpr/dot_general | solution.py:39
  150.4 2.8 %multiply_convert_fusion.3 = bf16[2048,256]{1,0:T(8,128)(2,1)} fusion(f32[2048,256]{1,0:T(8,128)S(1)} %get-tuple-element.215, bf16[128,256]{1,0:T(8,128)(2,1)S(1)} %get-tuple-element.214, bf16[2048,2048]{1,0:T(8,128)(2,1)} %get-tuple-element.213, s32[]{:T(128)S(6)} %select_n.23), kind=kOutput, calls=%fused_computation.4.clone.1 | convolution fusion | flops 137363456 | bytes 3735556 | tf_op jit(solution)/shard_map/while/body/eval_jaxpr/dot_general | solution.py:34
  153.2 2.0 %fusion.29 = f32[1,2048]{1,0:T(1,128)S(1)} fusion(bf16[256,1]{0,1:T(2,128)(2,1)S(1)} %reshape.77, bf16[2048,256]{1,0:T(8,128)(2,1)} %multiply_convert_fusion.3, bf16[256,256]{1,0:T(8,128)(2,1)S(1)} %get-tuple-element.216, f32[256]{0:T(256)S(1)} %get-tuple-element.217), kind=kOutput, calls=%fused_computation.5.clone.1 | convolution fusion | flops 272629760 | bytes 1189376 | tf_op jit(solution)/shard_map/while/body/eval_jaxpr/dot_general | solution.py:39
  156.7 2.8 %multiply_convert_fusion.3 = bf16[2048,256]{1,0:T(8,128)(2,1)} fusion(f32[2048,256]{1,0:T(8,128)S(1)} %get-tuple-element.215, bf16[128,256]{1,0:T(8,128)(2,1)S(1)} %get-tuple-element.214, bf16[2048,2048]{1,0:T(8,128)(2,1)} %get-tuple-element.213, s32[]{:T(128)S(6)} %select_n.23), kind=kOutput, calls=%fused_computation.4.clone.1 | convolution fusion | flops 137363456 | bytes 3735556 | tf_op jit(solution)/shard_map/while/body/eval_jaxpr/dot_general | solution.py:34
  159.5 2.0 %fusion.29 = f32[1,2048]{1,0:T(1,128)S(1)} fusion(bf16[256,1]{0,1:T(2,128)(2,1)S(1)} %reshape.77, bf16[2048,256]{1,0:T(8,128)(2,1)} %multiply_convert_fusion.3, bf16[256,256]{1,0:T(8,128)(2,1)S(1)} %get-tuple-element.216, f32[256]{0:T(256)S(1)} %get-tuple-element.217), kind=kOutput, calls=%fused_computation.5.clone.1 | convolution fusion | flops 272629760 | bytes 1189376 | tf_op jit(solution)/shard_map/while/body/eval_jaxpr/dot_general | solution.py:39
  161.7 0.8 fusion.7
  162.6 2.0 multiply_reduce_fusion
  165.3 39.0 %all-reduce.1 = (f32[2048]{0:T(1024)}, f32[]{:T(128)}) all-reduce(f32[2048]{0:T(1024)S(1)} %neg.21, f32[]{:T(128)S(6)} %neg.22), channel_id=1, replica_groups=mesh['mkt'=8,'trade'=1,'scen'=4] {'mkt','scen'}, use_global_device_ids=true, to_apply=%region_3.4 | all-reduce | flops 2049 | bytes 16392 | tf_op jit(solution)/shard_map/psum | solution.py:47
  (100 shorter events, 19.1 us)
Async XLA Ops:
  0.6 33.4 %copy-start = (bf16[16,128,128]{2,1,0:T(8,128)(2,1)S(1)}, bf16[16,128,128]{2,1,0:T(8,128)(2,1)}, u32[]{:S(2)}) copy-start(bf16[16,128,128]{2,1,0:T(8,128)(2,1)} %param.13) | copy-start | bytes 1572868
  34.4 8.9 %copy-start.2 = (s32[2048]{0:T(1024)S(1)}, s32[2048]{0:T(1024)}, u32[]{:S(2)}) copy-start(s32[2048]{0:T(1024)} %param.14) | copy-start | bytes 24580
  35.2 14.9 %all-to-all-start = ((bf16[16,4,2048]{2,0,1:T(8,128)(2,1)}), bf16[16,4,2048]{2,0,1:T(8,128)(2,1)S(1)}, u32[]{:S(2)}, u32[]{:S(2)}) async-start(bf16[16,4,2048]{2,0,1:T(8,128)(2,1)} %copy.14), calls=%async_computation | async-start | bytes 524288 | tf_op jit(solution)/shard_map/all_to_all | solution.py:26
  50.1 11.0 %copy-start.4 = (bf16[256,256]{1,0:T(8,128)(2,1)S(1)}, bf16[256,256]{1,0:T(8,128)(2,1)}, u32[]{:S(2)}) copy-start(bf16[256,256]{1,0:T(8,128)(2,1)} %param.19) | copy-start | bytes 393220
  50.1 11.0 %copy-start.5 = (bf16[128,256]{1,0:T(8,128)(2,1)S(1)}, bf16[128,256]{1,0:T(8,128)(2,1)}, u32[]{:S(2)}) copy-start(bf16[128,256]{1,0:T(8,128)(2,1)} %param.18) | copy-start | bytes 196612
  50.1 11.0 %copy-start.6 = (f32[256]{0:T(256)S(1)}, f32[256]{0:T(256)}, u32[]{:S(2)}) copy-start(f32[256]{0:T(256)} %param.20) | copy-start | bytes 3076
  50.2 11.0 %copy-start.7 = (bf16[256]{0:T(256)(128)(2,1)S(1)}, bf16[256]{0:T(256)(128)(2,1)}, u32[]{:S(2)}) copy-start(bf16[256]{0:T(256)(128)(2,1)} %param.21) | copy-start | bytes 1540
  61.1 100.6 %copy-start.3 = (s32[16]{0:T(128)S(1)}, s32[16]{0:T(128)}, u32[]{:S(2)}) copy-start(s32[16]{0:T(128)} %param.17) | copy-start | bytes 196
  61.2 101.4 %copy-start.1 = (f32[2048]{0:T(1024)S(1)}, f32[2048]{0:T(1024)}, u32[]{:S(2)}) copy-start(f32[2048]{0:T(1024)} %param.16) | copy-start | bytes 24580
where the time goes:
time: 207 us; the launch traced here: 204 us
  matrix products  80.6 us (39%)
  local copies, waits for them, and re-layouts  57.4 us (28%)
  blocking collectives  39 us (19%)
  loops' own time  10.9 us (5%)
  waiting for transfers between devices  6.9 us (3%)
  starting transfers between devices  6.02 us (3%)
    dot_general x16, matrix products, price(): jnp.dot(trade_rows, w_in, preferred_element_type=jnp.float32) + embed_float  44.7 us
    psum x1, blocking collectives, local(): lax.psum(-jnp.dot(weights, values, precision=lax.Precision.HIGHEST), ('mk...  39 us
    gather x48, local copies, waits for them, and re-layouts  33.3 us
    dot_general x16, matrix products, price(): return jnp.dot(hidden_two, w_out, preferred_element_type=jnp.float32)  32.7 us
    gather x1, local copies, waits for them, and re-layouts, local(): trade_rows_all = table[trade_block]  11 us
    another operation x1, loops' own time, local(): values = lax.map(price, jnp.arange(scen_count, dtype=jnp.int32))  10.9 us
    dynamic_slice x16, local copies, waits for them, and re-layouts, local(): values = lax.map(price, jnp.arange(scen_count, dtype=jnp.int32))  9.38 us
    all_to_all x1, waiting for transfers between devices, local(): lax.all_to_all(built_state, 'scen', split_axis=1, concat_axis=0, tiled=True)  6.9 us
  transfers between devices with their start and end apart: 1, of which 1 were waited for; matrix products, arithmetic and copies ran while one was open for 1% of the time, Pallas kernels for 0%

commit v1 on v0

--- a/solution.py
+++ b/solution.py
@@ -44,7 +44,10 @@
     weight_sum = jnp.sum(jnp.exp(-jnp.arange(scen_total, dtype=jnp.float32) / decay_span))
     weights = jnp.exp(-scen_rank.astype(jnp.float32) / decay_span) / weight_sum
     pnl_part = jnp.dot(values, position, precision=lax.Precision.HIGHEST)
-    marginal = lax.psum(-jnp.dot(weights, values, precision=lax.Precision.HIGHEST), ("mkt", "scen"))
+    marginal = jnp.sum(
+        lax.all_gather(-jnp.dot(weights, values, precision=lax.Precision.HIGHEST), ("mkt", "scen")),
+        axis=0,
+    )
     book_pnl = lax.psum(pnl_part, "trade")
     local_tail = -jnp.dot(weights, book_pnl, precision=lax.Precision.HIGHEST)
     shortfall = lax.psum(local_tail, ("mkt", "scen"))

time: 207 us -> 276 us (1.33)
  blocking collectives: 39 us -> 106 us
    all_gather x0 -> x1, blocking collectives: none -> 67.7 us  [local(): lax.all_gather(-jnp.dot(weights, values, precision=lax.Precision.HIGHEST)...]
where the time goes in v1:
time: 276 us; the launch traced here: 273 us
  blocking collectives  106 us (38%)
  matrix products  80.7 us (29%)
  local copies, waits for them, and re-layouts  57.4 us (21%)
  loops' own time  10.9 us (4%)
  waiting for transfers between devices  6.9 us (2%)
  starting transfers between devices  6.02 us (2%)
    all_gather x1, blocking collectives, local(): lax.all_gather(-jnp.dot(weights, values, precision=lax.Precision.HIGHEST)...  67.7 us
    dot_general x16, matrix products, price(): jnp.dot(trade_rows, w_in, preferred_element_type=jnp.float32) + embed_float  44.8 us
    psum x1, blocking collectives, local(): shortfall = lax.psum(local_tail, ('mkt', 'scen'))  38.8 us
    gather x48, local copies, waits for them, and re-layouts  33.3 us
    dot_general x16, matrix products, price(): return jnp.dot(hidden_two, w_out, preferred_element_type=jnp.float32)  32.7 us
    gather x1, local copies, waits for them, and re-layouts, local(): trade_rows_all = table[trade_block]  10.9 us
    another operation x1, loops' own time, local(): values = lax.map(price, jnp.arange(scen_count, dtype=jnp.int32))  10.9 us
    dynamic_slice x16, local copies, waits for them, and re-layouts, local(): values = lax.map(price, jnp.arange(scen_count, dtype=jnp.int32))  9.38 us
  transfers between devices with their start and end apart: 1, of which 1 were waited for; matrix products, arithmetic and copies ran while one was open for 1% of the time, Pallas kernels for 0%

profile of v1, /device:TPU:0, one launch (start us, length us, event | category | flops | bytes accessed | tf_op | source)
XLA Modules:
  0.0 272.5 jit_solution(18367021411751131644)
XLA Ops:
  0.7 33.3 %while.12 = (s32[]{:T(128)}, bf16[64,512]{1,0:T(8,128)(2,1)}, s32[16,2]{0,1:T(2,128)S(1)}, bf16[16,64,128]{2,1,0:T(8,128)(2,1)S(1)}, s32[]{:T(128)}) while((s32[]{:T(128)}, bf16[64,512]{1,0:T(8,128)(2,1)}, s32[16,2]{0,1:T(2,128)S(1)}, bf16[16,64,128]{2,1,0:T(8,128)(2,1)S(1)}, s32[]{:T(128)}) %tuple.34), condition=%wide.while_cond, body=%wide.while_body.sunk | while | flops 2 | bytes 32865 | solution.py:20
  1.3 1.5 bitcast_dynamic-update-slice_fusion.2
  3.4 1.5 bitcast_dynamic-update-slice_fusion.2
  5.5 1.5 bitcast_dynamic-update-slice_fusion.2
  7.5 1.5 bitcast_dynamic-update-slice_fusion.2
  9.6 1.5 bitcast_dynamic-update-slice_fusion.2
  11.7 1.5 bitcast_dynamic-update-slice_fusion.2
  13.8 1.5 bitcast_dynamic-update-slice_fusion.2
  15.9 1.5 bitcast_dynamic-update-slice_fusion.2
  17.9 1.5 bitcast_dynamic-update-slice_fusion.2
  20.0 1.5 bitcast_dynamic-update-slice_fusion.2
  22.1 1.5 bitcast_dynamic-update-slice_fusion.2
  24.2 1.5 bitcast_dynamic-update-slice_fusion.2
  26.3 1.5 bitcast_dynamic-update-slice_fusion.2
  28.3 1.5 bitcast_dynamic-update-slice_fusion.2
  30.4 1.5 bitcast_dynamic-update-slice_fusion.2
  32.5 1.5 bitcast_dynamic-update-slice_fusion.2
  34.4 0.8 copy.15
  35.2 6.0 %all-to-all-start = ((bf16[16,4,2048]{2,0,1:T(8,128)(2,1)}), bf16[16,4,2048]{2,0,1:T(8,128)(2,1)S(1)}, u32[]{:S(2)}, u32[]{:S(2)}) async-start(bf16[16,4,2048]{2,0,1:T(8,128)(2,1)} %copy.15), calls=%async_computation | async-start | bytes 524288 | tf_op jit(solution)/shard_map/all_to_all | solution.py:26
  41.2 1.4 convert_element_type.16
  42.6 0.6 exponential_reduce_fusion
  43.2 6.9 %all-to-all-done = bf16[16,4,2048]{2,0,1:T(8,128)(2,1)S(1)} async-done(((bf16[16,4,2048]{2,0,1:T(8,128)(2,1)}), bf16[16,4,2048]{2,0,1:T(8,128)(2,1)S(1)}, u32[]{:S(2)}, u32[]{:S(2)}) %all-to-all-start) | async-done | bytes 262176 | tf_op jit(solution)/shard_map/all_to_all | solution.py:26
  50.1 10.9 %gather_fusion = bf16[2048,2048]{1,0:T(8,128)(2,1)} fusion(bf16[64,2048]{1,0:T(8,128)(2,1)S(1)} %bitcast.38, s32[2048]{0:T(1024)S(1)} %fusion.6), kind=kCustom, calls=%fused_computation | custom fusion | bytes 16785408 | tf_op jit(solution)/shard_map/gather | solution.py:28
  61.1 100.6 %while.11 = (s32[]{:T(128)}, f32[16,2048]{1,0:T(8,128)S(1)}, s32[16]{0:T(128)S(1)}, bf16[2048,2048]{1,0:T(8,128)(2,1)}, bf16[128,256]{1,0:T(8,128)(2,1)S(1)}, /*...) while((s32[]{:T(128)}, f32[16,2048]{1,0:T(8,128)S(1)}, ...), condition=%wide.region_1.2_spmd, body=%wide.region_0.1_spmd.sunk | while | flops 409993216 | bytes 4942527 | solution.py:41
  61.2 0.6 dynamic_slice.12
  62.4 2.8 %multiply_convert_fusion.3 = bf16[2048,256]{1,0:T(8,128)(2,1)} fusion(f32[2048,256]{1,0:T(8,128)S(1)} %get-tuple-element.213, bf16[128,256]{1,0:T(8,128)(2,1)S(1)} %get-tuple-element.212, bf16[2048,2048]{1,0:T(8,128)(2,1)} %get-tuple-element.211, s32[]{:T(128)S(6)} %select_n.23), kind=kOutput, calls=%fused_computation.4.clone.1 | convolution fusion | flops 137363456 | bytes 3735556 | tf_op jit(solution)/shard_map/while/body/eval_jaxpr/dot_general | solution.py:34
  65.2 2.0 fusion.29
  67.4 0.6 dynamic_slice.12
  68.7 2.8 %multiply_convert_fusion.3 = bf16[2048,256]{1,0:T(8,128)(2,1)} fusion(f32[2048,256]{1,0:T(8,128)S(1)} %get-tuple-element.213, bf16[128,256]{1,0:T(8,128)(2,1)S(1)} %get-tuple-element.212, bf16[2048,2048]{1,0:T(8,128)(2,1)} %get-tuple-element.211, s32[]{:T(128)S(6)} %select_n.23), kind=kOutput, calls=%fused_computation.4.clone.1 | convolution fusion | flops 137363456 | bytes 3735556 | tf_op jit(solution)/shard_map/while/body/eval_jaxpr/dot_general | solution.py:34
  71.5 2.0 fusion.29
  73.7 0.6 dynamic_slice.12
  75.0 2.8 %multiply_convert_fusion.3 = bf16[2048,256]{1,0:T(8,128)(2,1)} fusion(f32[2048,256]{1,0:T(8,128)S(1)} %get-tuple-element.213, bf16[128,256]{1,0:T(8,128)(2,1)S(1)} %get-tuple-element.212, bf16[2048,2048]{1,0:T(8,128)(2,1)} %get-tuple-element.211, s32[]{:T(128)S(6)} %select_n.23), kind=kOutput, calls=%fused_computation.4.clone.1 | convolution fusion | flops 137363456 | bytes 3735556 | tf_op jit(solution)/shard_map/while/body/eval_jaxpr/dot_general | solution.py:34
  77.8 2.0 fusion.29
  81.3 2.8 %multiply_convert_fusion.3 = bf16[2048,256]{1,0:T(8,128)(2,1)} fusion(f32[2048,256]{1,0:T(8,128)S(1)} %get-tuple-element.213, bf16[128,256]{1,0:T(8,128)(2,1)S(1)} %get-tuple-element.212, bf16[2048,2048]{1,0:T(8,128)(2,1)} %get-tuple-element.211, s32[]{:T(128)S(6)} %select_n.23), kind=kOutput, calls=%fused_computation.4.clone.1 | convolution fusion | flops 137363456 | bytes 3735556 | tf_op jit(solution)/shard_map/while/body/eval_jaxpr/dot_general | solution.py:34
  84.1 2.0 fusion.29
  87.6 2.8 %multiply_convert_fusion.3 = bf16[2048,256]{1,0:T(8,128)(2,1)} fusion(f32[2048,256]{1,0:T(8,128)S(1)} %get-tuple-element.213, bf16[128,256]{1,0:T(8,128)(2,1)S(1)} %get-tuple-element.212, bf16[2048,2048]{1,0:T(8,128)(2,1)} %get-tuple-element.211, s32[]{:T(128)S(6)} %select_n.23), kind=kOutput, calls=%fused_computation.4.clone.1 | convolution fusion | flops 137363456 | bytes 3735556 | tf_op jit(solution)/shard_map/while/body/eval_jaxpr/dot_general | solution.py:34
  90.4 2.0 fusion.29
  93.8 2.8 %multiply_convert_fusion.3 = bf16[2048,256]{1,0:T(8,128)(2,1)} fusion(f32[2048,256]{1,0:T(8,128)S(1)} %get-tuple-element.213, bf16[128,256]{1,0:T(8,128)(2,1)S(1)} %get-tuple-element.212, bf16[2048,2048]{1,0:T(8,128)(2,1)} %get-tuple-element.211, s32[]{:T(128)S(6)} %select_n.23), kind=kOutput, calls=%fused_computation.4.clone.1 | convolution fusion | flops 137363456 | bytes 3735556 | tf_op jit(solution)/shard_map/while/body/eval_jaxpr/dot_general | solution.py:34
  96.7 2.0 fusion.29
  100.1 2.8 %multiply_convert_fusion.3 = bf16[2048,256]{1,0:T(8,128)(2,1)} fusion(f32[2048,256]{1,0:T(8,128)S(1)} %get-tuple-element.213, bf16[128,256]{1,0:T(8,128)(2,1)S(1)} %get-tuple-element.212, bf16[2048,2048]{1,0:T(8,128)(2,1)} %get-tuple-element.211, s32[]{:T(128)S(6)} %select_n.23), kind=kOutput, calls=%fused_computation.4.clone.1 | convolution fusion | flops 137363456 | bytes 3735556 | tf_op jit(solution)/shard_map/while/body/eval_jaxpr/dot_general | solution.py:34
  102.9 2.0 fusion.29
  106.4 2.8 %multiply_convert_fusion.3 = bf16[2048,256]{1,0:T(8,128)(2,1)} fusion(f32[2048,256]{1,0:T(8,128)S(1)} %get-tuple-element.213, bf16[128,256]{1,0:T(8,128)(2,1)S(1)} %get-tuple-element.212, bf16[2048,2048]{1,0:T(8,128)(2,1)} %get-tuple-element.211, s32[]{:T(128)S(6)} %select_n.23), kind=kOutput, calls=%fused_computation.4.clone.1 | convolution fusion | flops 137363456 | bytes 3735556 | tf_op jit(solution)/shard_map/while/body/eval_jaxpr/dot_general | solution.py:34
  109.2 2.0 fusion.29
  112.7 2.8 %multiply_convert_fusion.3 = bf16[2048,256]{1,0:T(8,128)(2,1)} fusion(f32[2048,256]{1,0:T(8,128)S(1)} %get-tuple-element.213, bf16[128,256]{1,0:T(8,128)(2,1)S(1)} %get-tuple-element.212, bf16[2048,2048]{1,0:T(8,128)(2,1)} %get-tuple-element.211, s32[]{:T(128)S(6)} %select_n.23), kind=kOutput, calls=%fused_computation.4.clone.1 | convolution fusion | flops 137363456 | bytes 3735556 | tf_op jit(solution)/shard_map/while/body/eval_jaxpr/dot_general | solution.py:34
  115.5 2.0 fusion.29
  119.0 2.8 %multiply_convert_fusion.3 = bf16[2048,256]{1,0:T(8,128)(2,1)} fusion(f32[2048,256]{1,0:T(8,128)S(1)} %get-tuple-element.213, bf16[128,256]{1,0:T(8,128)(2,1)S(1)} %get-tuple-element.212, bf16[2048,2048]{1,0:T(8,128)(2,1)} %get-tuple-element.211, s32[]{:T(128)S(6)} %select_n.23), kind=kOutput, calls=%fused_computation.4.clone.1 | convolution fusion | flops 137363456 | bytes 3735556 | tf_op jit(solution)/shard_map/while/body/eval_jaxpr/dot_general | solution.py:34
  121.8 2.0 fusion.29
  125.3 2.8 %multiply_convert_fusion.3 = bf16[2048,256]{1,0:T(8,128)(2,1)} fusion(f32[2048,256]{1,0:T(8,128)S(1)} %get-tuple-element.213, bf16[128,256]{1,0:T(8,128)(2,1)S(1)} %get-tuple-element.212, bf16[2048,2048]{1,0:T(8,128)(2,1)} %get-tuple-element.211, s32[]{:T(128)S(6)} %select_n.23), kind=kOutput, calls=%fused_computation.4.clone.1 | convolution fusion | flops 137363456 | bytes 3735556 | tf_op jit(solution)/shard_map/while/body/eval_jaxpr/dot_general | solution.py:34
  128.1 2.0 fusion.29
  131.6 2.8 %multiply_convert_fusion.3 = bf16[2048,256]{1,0:T(8,128)(2,1)} fusion(f32[2048,256]{1,0:T(8,128)S(1)} %get-tuple-element.213, bf16[128,256]{1,0:T(8,128)(2,1)S(1)} %get-tuple-element.212, bf16[2048,2048]{1,0:T(8,128)(2,1)} %get-tuple-element.211, s32[]{:T(128)S(6)} %select_n.23), kind=kOutput, calls=%fused_computation.4.clone.1 | convolution fusion | flops 137363456 | bytes 3735556 | tf_op jit(solution)/shard_map/while/body/eval_jaxpr/dot_general | solution.py:34
  134.4 2.0 fusion.29
  137.9 2.8 %multiply_convert_fusion.3 = bf16[2048,256]{1,0:T(8,128)(2,1)} fusion(f32[2048,256]{1,0:T(8,128)S(1)} %get-tuple-element.213, bf16[128,256]{1,0:T(8,128)(2,1)S(1)} %get-tuple-element.212, bf16[2048,2048]{1,0:T(8,128)(2,1)} %get-tuple-element.211, s32[]{:T(128)S(6)} %select_n.23), kind=kOutput, calls=%fused_computation.4.clone.1 | convolution fusion | flops 137363456 | bytes 3735556 | tf_op jit(solution)/shard_map/while/body/eval_jaxpr/dot_general | solution.py:34
  140.7 2.0 fusion.29
  144.2 2.8 %multiply_convert_fusion.3 = bf16[2048,256]{1,0:T(8,128)(2,1)} fusion(f32[2048,256]{1,0:T(8,128)S(1)} %get-tuple-element.213, bf16[128,256]{1,0:T(8,128)(2,1)S(1)} %get-tuple-element.212, bf16[2048,2048]{1,0:T(8,128)(2,1)} %get-tuple-element.211, s32[]{:T(128)S(6)} %select_n.23), kind=kOutput, calls=%fused_computation.4.clone.1 | convolution fusion | flops 137363456 | bytes 3735556 | tf_op jit(solution)/shard_map/while/body/eval_jaxpr/dot_general | solution.py:34
  147.0 2.0 fusion.29
  150.5 2.8 %multiply_convert_fusion.3 = bf16[2048,256]{1,0:T(8,128)(2,1)} fusion(f32[2048,256]{1,0:T(8,128)S(1)} %get-tuple-element.213, bf16[128,256]{1,0:T(8,128)(2,1)S(1)} %get-tuple-element.212, bf16[2048,2048]{1,0:T(8,128)(2,1)} %get-tuple-element.211, s32[]{:T(128)S(6)} %select_n.23), kind=kOutput, calls=%fused_computation.4.clone.1 | convolution fusion | flops 137363456 | bytes 3735556 | tf_op jit(solution)/shard_map/while/body/eval_jaxpr/dot_general | solution.py:34
  153.3 2.0 fusion.29
  156.8 2.8 %multiply_convert_fusion.3 = bf16[2048,256]{1,0:T(8,128)(2,1)} fusion(f32[2048,256]{1,0:T(8,128)S(1)} %get-tuple-element.213, bf16[128,256]{1,0:T(8,128)(2,1)S(1)} %get-tuple-element.212, bf16[2048,2048]{1,0:T(8,128)(2,1)} %get-tuple-element.211, s32[]{:T(128)S(6)} %select_n.23), kind=kOutput, calls=%fused_computation.4.clone.1 | convolution fusion | flops 137363456 | bytes 3735556 | tf_op jit(solution)/shard_map/while/body/eval_jaxpr/dot_general | solution.py:34
  159.6 2.0 fusion.29
  161.8 2.0 multiply_reduce_fusion
  164.5 0.8 fusion.7
  165.3 38.8 %psum.6 = f32[]{:T(128)} all-reduce(f32[]{:T(128)S(6)} %neg.22), channel_id=1, replica_groups=mesh['mkt'=8,'trade'=1,'scen'=4] {'mkt','scen'}, use_global_device_ids=true, to_apply=%region_4.5 | all-reduce | flops 1 | bytes 8 | tf_op jit(solution)/shard_map/psum | solution.py:53
  204.2 67.7 %all-gather = f32[65536]{0:T(1024)S(1)} all-gather(f32[2048]{0:T(1024)S(1)} %neg.21), channel_id=2, replica_groups=mesh['mkt'=8,'trade'=1,'scen'=4] {'mkt','scen'}, dimensions={0}, use_global_device_ids=true | all-gather | bytes 270336 | tf_op jit(solution)/shard_map/all_gather | solution.py:48
  271.9 0.6 reduce_sum.19
  (103 shorter events, 20.3 us)
Async XLA Ops:
  0.6 33.4 %copy-start = (bf16[16,128,128]{2,1,0:T(8,128)(2,1)S(1)}, bf16[16,128,128]{2,1,0:T(8,128)(2,1)}, u32[]{:S(2)}) copy-start(bf16[16,128,128]{2,1,0:T(8,128)(2,1)} %param.13) | copy-start | bytes 1572868
  34.4 8.9 %copy-start.2 = (s32[2048]{0:T(1024)S(1)}, s32[2048]{0:T(1024)}, u32[]{:S(2)}) copy-start(s32[2048]{0:T(1024)} %param.14) | copy-start | bytes 24580
  35.2 14.9 %all-to-all-start = ((bf16[16,4,2048]{2,0,1:T(8,128)(2,1)}), bf16[16,4,2048]{2,0,1:T(8,128)(2,1)S(1)}, u32[]{:S(2)}, u32[]{:S(2)}) async-start(bf16[16,4,2048]{2,0,1:T(8,128)(2,1)} %copy.15), calls=%async_computation | async-start | bytes 524288 | tf_op jit(solution)/shard_map/all_to_all | solution.py:26
  50.1 11.0 %copy-start.4 = (bf16[256,256]{1,0:T(8,128)(2,1)S(1)}, bf16[256,256]{1,0:T(8,128)(2,1)}, u32[]{:S(2)}) copy-start(bf16[256,256]{1,0:T(8,128)(2,1)} %param.19) | copy-start | bytes 393220
  50.1 11.0 %copy-start.5 = (bf16[128,256]{1,0:T(8,128)(2,1)S(1)}, bf16[128,256]{1,0:T(8,128)(2,1)}, u32[]{:S(2)}) copy-start(bf16[128,256]{1,0:T(8,128)(2,1)} %param.18) | copy-start | bytes 196612
  50.1 11.0 %copy-start.6 = (f32[256]{0:T(256)S(1)}, f32[256]{0:T(256)}, u32[]{:S(2)}) copy-start(f32[256]{0:T(256)} %param.20) | copy-start | bytes 3076
  50.1 11.0 %copy-start.7 = (bf16[256]{0:T(256)(128)(2,1)S(1)}, bf16[256]{0:T(256)(128)(2,1)}, u32[]{:S(2)}) copy-start(bf16[256]{0:T(256)(128)(2,1)} %param.21) | copy-start | bytes 1540
  61.1 100.7 %copy-start.1 = (f32[2048]{0:T(1024)S(1)}, f32[2048]{0:T(1024)}, u32[]{:S(2)}) copy-start(f32[2048]{0:T(1024)} %param.16) | copy-start | bytes 24580
  61.1 100.7 %copy-start.3 = (s32[16]{0:T(128)S(1)}, s32[16]{0:T(128)}, u32[]{:S(2)}) copy-start(s32[16]{0:T(128)} %param.17) | copy-start | bytes 196
